TPU v7x, 32 devices: a whole 2x2x4 slice. The times are simulated.
32 devices in a mesh: expert: 8 (over z, y), half: 4 (over x, core).
Axes of the slice: x: 2, y: 2, z: 4, core: 2. Of those that a mesh axis runs over, the one named last changes fastest.
Arguments:
- tokens: bfloat16 [1024, 2048], P('expert', 'half'), may hold values from -6 to 6
- cotangent: bfloat16 [1024, 2048], P('expert', 'half'), may hold values from -4 to 4
- route: int32 [1024, 8], P('expert'), may hold values from 0 to 15, all different within a row; in each aligned block of 128 rows (0 to 127, 128 to 255, ...) at most 128 rows name the same one
- prob: bfloat16 [1024, 8], P('expert'), may hold values from 0.19921875 to 1
- w_gate: bfloat16 [16, 768, 2048], P('expert', 'half'), may hold values from -0.125 to 0.125
- w_up: bfloat16 [16, 768, 2048], P('expert', 'half'), may hold values from -0.125 to 0.125
- w_down: bfloat16 [16, 768, 2048], P('expert', 'half'), may hold values from -0.21875 to 0.21875
Outputs:
- grad_tokens: bfloat16 [1024, 2048], P('expert', 'half')
- grad_prob: float32 [1024, 8], P('expert')
- grad_gate: bfloat16 [16, 768, 2048], P('expert', 'half')
- grad_up: bfloat16 [16, 768, 2048], P('expert', 'half')
- grad_down: bfloat16 [16, 768, 2048], P('expert', 'half')
Inputs may be any that keep to these rules, and one draw needn't show every extreme that they name: `route`: each row names 8 different experts; among the rows of one device no expert is named more than 128 times, and that most is reached.
All inputs are finite; a program needn't handle non-finite values.
Results may differ from a plain program's by a relative error of at most 0.013.
Values may be sent and summed in bfloat16 or wider, within the bound.
A program may use at most 192 MiB of HBM per device.

v0:
```python
import jax
import jax.numpy as jnp
from jax import lax
from jax.sharding import PartitionSpec as P


def per_device(tokens, cotangent, route, prob, w_gate, w_up, w_down):
    tok_rows = route.shape[0]
    top = route.shape[1]
    local_exp = w_gate.shape[0]
    groups = lax.axis_size("expert")
    experts = local_exp * groups
    capacity = 2 * tok_rows * top // experts
    slots = experts * capacity
    flat_route = route.reshape(-1)
    hits = (flat_route[:, None] == jnp.arange(experts, dtype=jnp.int32)[None, :]).astype(jnp.int32)
    rank = jnp.sum((jnp.cumsum(hits, axis=0) - hits) * hits, axis=1)
    slot_of = flat_route * capacity + rank
    source = (
        jnp.zeros((slots,), jnp.int32).at[slot_of].set(jnp.arange(tok_rows * top, dtype=jnp.int32))
    )
    filled = jnp.zeros((slots,), jnp.bool_).at[slot_of].set(True)
    token_of = source // top
    slot_prob = jnp.where(filled, prob.reshape(-1)[source], jnp.zeros((), jnp.bfloat16))
    slot_prob = slot_prob.reshape(groups, local_exp * capacity)

    def pack(rows):
        picked = jnp.where(filled[:, None], rows[token_of], jnp.zeros((), jnp.bfloat16))
        return picked.reshape(groups, local_exp * capacity, rows.shape[1])

    sent_x, sent_d, recv_p = (
        lax.all_to_all(pack(tokens), "expert", split_axis=0, concat_axis=0, tiled=True),
        lax.all_to_all(pack(cotangent), "expert", split_axis=0, concat_axis=0, tiled=True),
        lax.all_to_all(slot_prob, "expert", split_axis=0, concat_axis=0, tiled=True),
    )
    recv_x, recv_d = (
        lax.all_gather(sent_x, "half", axis=2, tiled=True),
        lax.all_gather(sent_d, "half", axis=2, tiled=True),
    )
    width = recv_x.shape[2]
    xin = recv_x.reshape(groups, local_exp, capacity, width)
    dout = recv_d.reshape(groups, local_exp, capacity, width)
    weight = recv_p.reshape(groups, local_exp, capacity).astype(jnp.float32)
    gate = jnp.einsum("gecd,efd->gecf", xin, w_gate, preferred_element_type=jnp.float32)
    upval = jnp.einsum("gecd,efd->gecf", xin, w_up, preferred_element_type=jnp.float32)
    sig = jax.nn.sigmoid(gate)
    act = gate * sig
    hidden = (act * upval).astype(jnp.bfloat16)
    raw = jnp.einsum("gecd,efd->gecf", dout, w_down, preferred_element_type=jnp.float32)
    score = jnp.sum(hidden.astype(jnp.float32) * raw, axis=3)
    scaled = (weight[..., None] * dout.astype(jnp.float32)).astype(jnp.bfloat16)
    dact = weight[..., None] * raw
    dgate = (dact * upval * sig * (1.0 + gate * (1.0 - sig))).astype(jnp.bfloat16)
    dup = (dact * act).astype(jnp.bfloat16)
    grad_down = jnp.einsum(
        "gecf,gecd->efd", hidden, scaled, preferred_element_type=jnp.float32
    ).astype(jnp.bfloat16)
    grad_gate = jnp.einsum("gecf,gecd->efd", dgate, xin, preferred_element_type=jnp.float32).astype(
        jnp.bfloat16
    )
    grad_up = jnp.einsum("gecf,gecd->efd", dup, xin, preferred_element_type=jnp.float32).astype(
        jnp.bfloat16
    )
    part = jnp.einsum("gecf,efd->gecd", dgate, w_gate, preferred_element_type=jnp.float32)
    part = (
        part + jnp.einsum("gecf,efd->gecd", dup, w_up, preferred_element_type=jnp.float32)
    ).astype(jnp.bfloat16)
    summed = lax.psum_scatter(
        part.astype(jnp.float32).astype(jnp.bfloat16), "half", scatter_dimension=3, tiled=True
    ).astype(jnp.float32)
    total_score = lax.psum(score, "half")
    quarter = summed.shape[3]
    back_rows, back_score = (
        lax.all_to_all(
            summed.reshape(groups, local_exp * capacity, quarter).astype(jnp.bfloat16),
            "expert",
            split_axis=0,
            concat_axis=0,
            tiled=True,
        ).astype(jnp.float32),
        lax.all_to_all(
            total_score.reshape(groups, local_exp * capacity).astype(jnp.bfloat16),
            "expert",
            split_axis=0,
            concat_axis=0,
            tiled=True,
        ).astype(jnp.float32),
    )
    picked = back_rows.reshape(slots, quarter)[slot_of].reshape(tok_rows, top, quarter)
    grad_tokens = jnp.sum(picked, axis=1).astype(jnp.bfloat16)
    grad_prob = back_score.reshape(slots)[slot_of].reshape(tok_rows, top)
    return (grad_tokens, grad_prob, grad_gate, grad_up, grad_down)


def solution(mesh):
    in_specs = (
        P("expert", "half"),
        P("expert", "half"),
        P("expert", None),
        P("expert", None),
        P("expert", "half", None),
        P("expert", "half", None),
        P("expert", "half", None),
    )
    out_specs = (
        P("expert", "half"),
        P("expert", None),
        P("expert", "half", None),
        P("expert", "half", None),
        P("expert", "half", None),
    )
    return jax.shard_map(
        per_device, mesh=mesh, in_specs=in_specs, out_specs=out_specs, check_vma=False
    )
```

profile of v0, /device:TPU:0, one launch (start us, length us, event | category | flops | bytes accessed | tf_op | source)
XLA Modules:
  0.0 395.6 jit_solution(12348937740041359488)
XLA Ops:
  9.2 4.5 %reduce-window.6 = s32[16,8,128]{2,1,0:T(8,128)S(1)} reduce-window(s32[16,8,128]{2,1,0:T(8,128)S(1)} %fusion.37, s32[]{:T(128)} %constant.15.clone.1), window={size=1x1x128 pad=0_0x0_0x127_0}, to_apply=%region_0.0 | reduce-window | flops 2080768 | bytes 131076 | tf_op jit(solution)/shard_map/reduce-window
  14.2 4.3 %scatter_custom_fusion = pred[2048]{0:T(1024)(128)(4,1)S(1)} fusion(s32[1024]{0:T(1024)S(1)} %bitcast.130, pred[1024]{0:T(1024)(128)(4,1)S(1)} %broadcast.70, pred[]{:T(512)} %constant.13.clone.1), kind=kCustom, calls=%fused_computation.76 | custom fusion | bytes 2049 | tf_op jit(solution)/shard_map/scatter | solution.py:22
  18.6 4.3 %scatter_custom_fusion.1 = s32[2048]{0:T(1024)S(1)} fusion(s32[1024]{0:T(1024)S(1)} %bitcast.131, s32[1024]{0:T(1024)S(1)} %iota.11, s32[]{:T(128)} %constant.15.clone.1), kind=kCustom, calls=%fused_computation.74 | custom fusion | bytes 8196 | tf_op jit(solution)/shard_map/scatter | solution.py:20
  23.0 9.2 %gather_fusion.2 = bf16[2048,512]{1,0:T(8,128)(2,1)} fusion(bf16[128,512]{1,0:T(8,128)(2,1)S(1)} %copy-done.2, s32[2048]{0:T(1024)S(1)} %get-tuple-element.25), kind=kCustom, calls=%fused_computation.2 | custom fusion | bytes 4202496 | tf_op jit(solution)/shard_map/gather | solution.py:28
  32.1 9.2 %gather_fusion.1 = bf16[2048,512]{1,0:T(8,128)(2,1)} fusion(bf16[128,512]{1,0:T(8,128)(2,1)S(1)} %copy-done.3, s32[2048]{0:T(1024)S(1)} %get-tuple-element.25), kind=kCustom, calls=%fused_computation.1 | custom fusion | bytes 4202496 | tf_op jit(solution)/shard_map/gather | solution.py:28
  44.7 55.4 %all_to_all.31 = bf16[8,256,512]{2,1,0:T(8,128)(2,1)} all-to-all(bf16[8,256,512]{2,1,0:T(8,128)(2,1)S(1)} %get-tuple-element.27), channel_id=1, replica_groups=mesh['expert'=8,'half'=4] {'expert'}, dimensions={0} | all-to-all | bytes 4194304 | tf_op jit(solution)/shard_map/all_to_all | solution.py:32
  100.2 51.8 %all_to_all.32 = bf16[8,256,512]{2,1,0:T(8,128)(2,1)} all-to-all(bf16[8,256,512]{2,1,0:T(8,128)(2,1)} %get-tuple-element.26), channel_id=1, replica_groups=mesh['expert'=8,'half'=4] {'expert'}, dimensions={0} | all-to-all | bytes 4194304 | tf_op jit(solution)/shard_map/all_to_all | solution.py:33
  152.9 13.1 %gather_fusion = bf16[2048]{0:T(1024)(128)(2,1)S(1)} fusion(bf16[1024]{0:T(1024)(128)(2,1)S(1)} %reshape.125, s32[2048]{0:T(1024)S(1)} %get-tuple-element.24), kind=kCustom, calls=%fused_computation | custom fusion | bytes 16384 | tf_op jit(solution)/shard_map/gather | solution.py:24
  167.2 9.8 %all_to_all.33 = bf16[8,2,128]{2,1,0:T(2,128)(2,1)S(1)} all-to-all(bf16[8,2,128]{2,1,0:T(2,128)(2,1)S(1)} %reshape.205), channel_id=1, replica_groups=mesh['expert'=8,'half'=4] {'expert'}, dimensions={0} | all-to-all | bytes 8192 | tf_op jit(solution)/shard_map/all_to_all | solution.py:34
  177.1 6.6 %fusion.9 = f32[2,8,128,192]{2,3,1,0:T(8,128)} fusion(bf16[8,2,128,2048]{3,2,1,0:T(8,128)(2,1)} %bitcast.134, bf16[2,192,2048]{2,1,0:T(8,128)(2,1)S(1)} %copy-done), kind=kOutput, calls=%fused_computation.18 | convolution fusion | flops 1610612736 | bytes 11534336 | tf_op jit(solution)/shard_map/gecd,efd->gecf/dot_general | solution.py:44
  187.8 29.7 %all-gather.3.cloned.1.call-done = bf16[8,256,2048]{2,1,0:T(8,128)(2,1)} async-done(((bf16[8,256,512]{2,1,0:T(8,128)(2,1)}), bf16[8,256,2048]{2,1,0:T(8,128)(2,1)}) %all-gather.3.cloned.1.call-update) | async-done | bytes 8388624 | tf_op jit(solution)/shard_map/all_gather | solution.py:38
  217.5 9.2 %fusion.33 = (f32[8,2,128]{2,0,1:T(8,128)S(1)}, bf16[8,2,128,192]{2,3,0,1:T(8,128)(2,1)}, bf16[8,2,128,192]{2,3,0,1:T(8,128)(2,1)S(1)}, bf16[8,2,128,192]{2,3,0,1:T(8,128)(2,1)S(1)}) fusion(f32[2,8,128,192]{2,3,1,0:T(8,128)} %fusion.11, f32[2,8,128,192]{2,3,1,0:T(8,128)} %fusion.9, f32[8,2,128]{2,0,1:T(8,128)S(1)} %bitcast_convert_fusion.4, ...), kind=kOutput, calls=%fused_computation.50 | convolution fusion | flops 1618081792 | bytes 15482880 | tf_op jit(solution)/shard_map/gecd,efd->gecf/dot_general | solution.py:49
  226.7 8.1 %fusion.19 = f32[2,8,128,2048]{3,2,1,0:T(8,128)} fusion(bf16[8,2,128,192]{2,3,0,1:T(8,128)(2,1)S(1)} %get-tuple-element.22, bf16[2,192,2048]{2,1,0:T(8,128)(2,1)S(1)} %copy-done), kind=kOutput, calls=%fused_computation.29 | convolution fusion | flops 1610612736 | bytes 19136512 | tf_op jit(solution)/shard_map/gecf,efd->gecd/dot_general | solution.py:64
  234.8 11.4 %fusion = bf16[8,2,128,2048]{3,2,0,1:T(8,128)(2,1)} fusion(f32[2,8,128,2048]{3,2,1,0:T(8,128)} %fusion.19, bf16[8,2,128,192]{2,3,0,1:T(8,128)(2,1)S(1)} %get-tuple-element.23, bf16[2,192,2048]{2,1,0:T(8,128)(2,1)S(1)} %copy-done.4), kind=kOutput, calls=%fused_computation.9 | convolution fusion | flops 1619001344 | bytes 27525120 | tf_op jit(solution)/shard_map/gecf,efd->gecd/dot_general | solution.py:66
  246.2 6.0 %psum.7 = bf16[8,2,128]{2,0,1:T(8,128)(2,1)S(1)} all-reduce(f32[8,2,128]{2,0,1:T(8,128)S(1)} %get-tuple-element.20), channel_id=1, replica_groups=mesh['expert'=8,'half'=4] {'half'}, use_global_device_ids=true, to_apply=%region_8.9 | all-reduce | flops 2048 | bytes 12288 | tf_op jit(solution)/shard_map/psum | solution.py:71
  253.5 5.7 %all-to-all-start.4 = ((bf16[8,2,128]{2,1,0:T(2,128)(2,1)}), bf16[8,2,128]{2,1,0:T(2,128)(2,1)S(1)}, u32[]{:S(2)}, u32[]{:S(2)}) async-start(bf16[8,2,128]{2,1,0:T(2,128)(2,1)} %reshape.207), calls=%async_computation.5 | async-start | bytes 8192 | tf_op jit(solution)/shard_map/all_to_all | solution.py:81
  259.1 58.4 %reduce-scatter.2.cloned.1.call-done = bf16[8,2,128,512]{3,2,0,1:T(8,128)(2,1)} async-done(((bf16[8,2,128,2048]{3,2,0,1:T(8,128)(2,1)}), bf16[8,2,128,512]{3,2,0,1:T(8,128)(2,1)}) %reduce-scatter.2.cloned.1.call-update) | async-done | bytes 2097168 | tf_op jit(solution)/shard_map/reduce_scatter | solution.py:68
  320.7 5.6 %all-to-all-start.3 = ((bf16[8,256,512]{2,1,0:T(8,128)(2,1)}), bf16[8,256,512]{2,1,0:T(8,128)(2,1)}, u32[]{:S(2)}, u32[]{:S(2)}) async-start(bf16[8,256,512]{2,1,0:T(8,128)(2,1)} %bitcast.126), calls=%async_computation.4 | async-start | bytes 4194304 | tf_op jit(solution)/shard_map/all_to_all | solution.py:74
  326.4 6.5 %bitcast_convert_fusion.2 = bf16[2,192,2048]{2,1,0:T(8,128)(2,1)} fusion(bf16[8,2,128,192]{2,3,0,1:T(8,128)(2,1)S(1)} %copy-done.6, bf16[8,2,128,2048]{3,2,1,0:T(8,128)(2,1)} %bitcast.135), kind=kOutput, calls=%fused_computation.24 | convolution fusion | flops 1611399168 | bytes 10747904 | tf_op jit(solution)/shard_map/gecf,gecd->efd/dot_general | solution.py:58
  332.9 6.5 %bitcast_convert_fusion.1 = bf16[2,192,2048]{2,1,0:T(8,128)(2,1)} fusion(bf16[8,2,128,192]{2,3,0,1:T(8,128)(2,1)S(1)} %copy-done.8, bf16[8,2,128,2048]{3,2,1,0:T(8,128)(2,1)} %bitcast.136), kind=kOutput, calls=%fused_computation.23 | convolution fusion | flops 1611399168 | bytes 10747904 | tf_op jit(solution)/shard_map/gecf,gecd->efd/dot_general | solution.py:61
  342.7 6.2 %gather_fusion.4 = f32[1024]{0:T(1024)S(1)} fusion(f32[2048]{0:T(1024)S(1)} %bitcast.123, s32[1024]{0:T(1024)S(1)} %broadcast_clamp_fusion), kind=kCustom, calls=%fused_computation.4 | custom fusion | bytes 12288 | tf_op jit(solution)/shard_map/gather | solution.py:91
  349.6 24.9 %all-to-all-done.3 = bf16[8,256,512]{2,1,0:T(8,128)(2,1)} async-done(((bf16[8,256,512]{2,1,0:T(8,128)(2,1)}), bf16[8,256,512]{2,1,0:T(8,128)(2,1)}, u32[]{:S(2)}, u32[]{:S(2)}) %all-to-all-start.3) | async-done | bytes 2097184 | tf_op jit(solution)/shard_map/all_to_all | solution.py:74
  374.5 4.1 %bitcast_convert_fusion.3 = f32[2048,512]{1,0:T(8,128)} fusion(bf16[8,256,512]{2,1,0:T(8,128)(2,1)} %all-to-all-done.3), kind=kLoop, calls=%fused_computation.25 | loop fusion | flops 1048576 | bytes 6291456 | tf_op jit(solution)/shard_map/reshape | solution.py:89
  378.6 7.6 %gather_fusion.3 = f32[1024,512]{1,0:T(8,128)} fusion(f32[2048,512]{1,0:T(8,128)} %bitcast_convert_fusion.3, s32[1024]{0:T(1024)S(1)} %broadcast_clamp_fusion), kind=kCustom, calls=%fused_computation.3 | custom fusion | bytes 4198400 | tf_op jit(solution)/shard_map/gather | solution.py:89
  (78 shorter events, 23.5 us)
Async XLA Ops:
  7.2 169.9 %copy-start = (bf16[2,192,2048]{2,1,0:T(8,128)(2,1)S(1)}, bf16[2,192,2048]{2,1,0:T(8,128)(2,1)}, u32[]{:S(2)}) copy-start(bf16[2,192,2048]{2,1,0:T(8,128)(2,1)} %param.11) | copy-start | bytes 4718596
  7.2 15.8 %copy-start.2 = (bf16[128,512]{1,0:T(8,128)(2,1)S(1)}, bf16[128,512]{1,0:T(8,128)(2,1)}, u32[]{:S(2)}) copy-start(bf16[128,512]{1,0:T(8,128)(2,1)} %param.7) | copy-start | bytes 393220
  7.2 169.8 %all-gather.5.cloned.1.call-start = ((), (), s32[]{:S(2)}) async-start(), calls=%async_computation.7 | async-start | bytes 10485760 | tf_op jit(solution)/shard_map/all_gather | solution.py:37
  23.0 9.2 %copy-start.3 = (bf16[128,512]{1,0:T(8,128)(2,1)S(1)}, bf16[128,512]{1,0:T(8,128)(2,1)}, u32[]{:S(2)}) copy-start(bf16[128,512]{1,0:T(8,128)(2,1)} %param.8) | copy-start | bytes 393220
  100.2 117.3 %all-gather.3.cloned.1.call-start = ((), (), s32[]{:S(2)}) async-start(), calls=%async_computation.6 | async-start | bytes 10485760 | tf_op jit(solution)/shard_map/all_gather | solution.py:38
  152.0 0.7 copy-start.9
  152.0 165.6 %reduce-scatter.2.cloned.1.call-start = ((), (), s32[]{:S(2)}) async-start(), calls=%async_computation.8 | async-start | bytes 10485760 | tf_op jit(solution)/shard_map/reduce_scatter | solution.py:68
  177.1 6.6 %copy-start.4 = (bf16[2,192,2048]{2,1,0:T(8,128)(2,1)S(1)}, bf16[2,192,2048]{2,1,0:T(8,128)(2,1)}, u32[]{:S(2)}) copy-start(bf16[2,192,2048]{2,1,0:T(8,128)(2,1)} %param.12) | copy-start | bytes 4718596
  177.1 6.6 %copy-start.10 = (bf16[8,256,2048]{2,1,0:T(8,128)(2,1)S(1)}, bf16[8,256,2048]{2,1,0:T(8,128)(2,1)}, u32[]{:S(2)}) copy-start(bf16[8,256,2048]{2,1,0:T(8,128)(2,1)} %all-gather.5.cloned.1.call-done) | copy-start | bytes 25165828
  226.7 8.1 %copy-start.5 = (bf16[8,2,128,192]{2,3,0,1:T(8,128)(2,1)}, bf16[8,2,128,192]{2,3,0,1:T(8,128)(2,1)S(1)}, u32[]{:S(2)}) copy-start(bf16[8,2,128,192]{2,3,0,1:T(8,128)(2,1)S(1)} %get-tuple-element.22) | copy-start | bytes 2359300
  226.7 8.1 %copy-start.7 = (bf16[8,2,128,192]{2,3,0,1:T(8,128)(2,1)}, bf16[8,2,128,192]{2,3,0,1:T(8,128)(2,1)S(1)}, u32[]{:S(2)}) copy-start(bf16[8,2,128,192]{2,3,0,1:T(8,128)(2,1)S(1)} %get-tuple-element.23) | copy-start | bytes 2359300
  253.5 67.3 %all-to-all-start.4 = ((bf16[8,2,128]{2,1,0:T(2,128)(2,1)}), bf16[8,2,128]{2,1,0:T(2,128)(2,1)S(1)}, u32[]{:S(2)}, u32[]{:S(2)}) async-start(bf16[8,2,128]{2,1,0:T(2,128)(2,1)} %reshape.207), calls=%async_computation.5 | async-start | bytes 8192 | tf_op jit(solution)/shard_map/all_to_all | solution.py:81
  320.7 5.7 %copy-start.6 = (bf16[8,2,128,192]{2,3,0,1:T(8,128)(2,1)S(1)}, bf16[8,2,128,192]{2,3,0,1:T(8,128)(2,1)}, u32[]{:S(2)}) copy-start(bf16[8,2,128,192]{2,3,0,1:T(8,128)(2,1)} %copy-done.5) | copy-start | bytes 2359300
  320.7 53.8 %all-to-all-start.3 = ((bf16[8,256,512]{2,1,0:T(8,128)(2,1)}), bf16[8,256,512]{2,1,0:T(8,128)(2,1)}, u32[]{:S(2)}, u32[]{:S(2)}) async-start(bf16[8,256,512]{2,1,0:T(8,128)(2,1)} %bitcast.126), calls=%async_computation.4 | async-start | bytes 4194304 | tf_op jit(solution)/shard_map/all_to_all | solution.py:74
  326.4 6.5 %copy-start.8 = (bf16[8,2,128,192]{2,3,0,1:T(8,128)(2,1)S(1)}, bf16[8,2,128,192]{2,3,0,1:T(8,128)(2,1)}, u32[]{:S(2)}) copy-start(bf16[8,2,128,192]{2,3,0,1:T(8,128)(2,1)} %copy-done.7) | copy-start | bytes 2359300
  326.4 13.0 %slice-start = ((s8[8388608]{0:T(1024)(128)(4,1)}), s8[4194304]{0:T(1024)(128)(4,1)S(1)}, s32[]{:S(2)}) async-start(s8[8388608]{0:T(1024)(128)(4,1)} %bitcast.139), calls=%async_computation.9 | async-start | bytes 8388608
  332.9 6.5 %slice-start.1 = ((s8[8388608]{0:T(1024)(128)(4,1)}), s8[4194304]{0:T(1024)(128)(4,1)S(1)}, s32[]{:S(2)}) async-start(s8[8388608]{0:T(1024)(128)(4,1)} %bitcast.139), calls=%async_computation.10 | async-start | bytes 8388608
  332.9 6.5 %copy-start.11 = (bf16[8,2,128,192]{2,3,0,1:T(8,128)(2,1)S(1)}, bf16[8,2,128,192]{2,3,0,1:T(8,128)(2,1)}, u32[]{:S(2)}) copy-start(bf16[8,2,128,192]{2,3,0,1:T(8,128)(2,1)} %get-tuple-element.21) | copy-start | bytes 2359300
  378.6 10.4 %copy-start.1 = (bf16[2,192,2048]{2,1,0:T(8,128)(2,1)S(1)}, bf16[2,192,2048]{2,1,0:T(8,128)(2,1)}, u32[]{:S(2)}) copy-start(bf16[2,192,2048]{2,1,0:T(8,128)(2,1)} %param.11) | copy-start | bytes 4718596
Sparse Core Ops, SparseCore 0:
  100.3 57.2 all-gather.4
  159.2 58.2 all-gather.2
  246.3 71.2 reduce-scatter.1
where the time goes:
time: 396 us
  blocking collectives  123 us (31%)
  waiting for transfers between devices  113 us (29%)
  local copies, waits for them, and re-layouts  61.2 us (15%)
  matrix products  55.6 us (14%)
  other arithmetic  17.2 us (4%)
  between operations  14 us (4%)
  starting transfers between devices  11.5 us (3%)
    reduce_scatter x1, waiting for transfers between devices, per_device(): lax.psum_scatter(part.astype(jnp.float32).astype(jnp.bfloat16), 'half', s...  58.4 us
    all_to_all x1, blocking collectives, per_device(): lax.all_to_all(pack(tokens), 'expert', split_axis=0, concat_axis=0, tiled...  55.4 us
    all_to_all x1, blocking collectives, per_device(): lax.all_to_all(pack(cotangent), 'expert', split_axis=0, concat_axis=0, ti...  51.8 us
    all_gather x1, waiting for transfers between devices, per_device(): lax.all_gather(sent_d, 'half', axis=2, tiled=True)  29.7 us
    all_to_all x1, waiting for transfers between devices, per_device(): lax.all_to_all(summed.reshape(groups, local_exp * capacity, quarter).asty...  24.9 us
    gather x2, local copies, waits for them, and re-layouts, pack(): rows[token_of]  18.3 us
    gather x1, local copies, waits for them, and re-layouts, per_device(): prob.reshape(-1)[source]  13.1 us
    dot_general x1, matrix products, per_device(): jnp.einsum('gecf,efd->gecd', dup, w_up, preferred_element_type=jnp.float32)  11.4 us
  transfers between devices with their start and end apart: 5, of which 3 were waited for; matrix products, arithmetic and copies ran while one was open for 13% of the time, Pallas kernels for 0%

commit v1 on v0

v1 whole, which is shorter than its diff:
```python
import functools

import jax
import jax.numpy as jnp
from jax import lax
from jax.experimental import pallas as pl
from jax.experimental.pallas import tpu as pltpu
from jax.sharding import PartitionSpec as P

BOTH = ("expert", "half")


def gather_all(block, groups, halves):
    rows, quarter = block.shape
    parts = lax.all_gather(block, BOTH, axis=0).reshape(groups, halves, rows, quarter)
    return parts.transpose(0, 2, 1, 3).reshape(groups * rows, halves * quarter)


LANES = 128
MESH = pl.DeviceIdType.MESH


def place(groups):
    e, h = lax.axis_index("expert"), lax.axis_index("half")
    return lax.div(e, 2), lax.rem(e, 2), lax.div(h, 2), lax.rem(h, 2)


def greet(peers):
    barrier = pltpu.get_barrier_semaphore()
    for peer in peers:
        pl.semaphore_signal(barrier, inc=1, device_id=peer, device_id_type=MESH)
    pl.semaphore_wait(barrier, len(peers))


def gather_kernel(
    groups, tok_ref, cot_ref, tab_ref, x_ref, d_ref, w_ref,
    send_sem, z_sem, p_sem, q_sem, c_sem, tab_send, tab_recv, own_sem,
):
    line = groups // 2
    z, y, x, c = place(groups)
    e, h = 2 * z + y, 2 * x + c
    rows, quarter = tok_ref.shape
    y_peer = (2 * z + 1 - y, h)
    x_peer = (e, 2 * (1 - x) + c)
    c_peer = (e, 2 * x + 1 - c)
    ring = [(lax.rem(e + s, groups), h) for s in range(1, groups)]
    greet(ring + [x_peer, c_peer])

    sends, owns = [], []

    def push(src, dst, peer, number, sem):
        copy = pltpu.make_async_remote_copy(
            src_ref=src, dst_ref=dst, send_sem=number, recv_sem=sem,
            device_id=peer, device_id_type=MESH,
        )
        copy.start()
        sends.append(copy)

    def slot(out, zz, yy, xx, cc):
        row = pl.multiple_of((2 * zz + yy) * rows, rows)
        col = pl.multiple_of((2 * xx + cc) * quarter, quarter)
        return out.at[pl.ds(row, rows), pl.ds(col, quarter)]

    arrays = []
    for a, (src, out) in enumerate(((tok_ref, x_ref), (cot_ref, d_ref))):
        first, second = (y_peer, x_peer) if a == 0 else (x_peer, y_peer)

        def at(step, kind, out=out, a=a):
            zz = lax.rem(z - step + line, line)
            flip_first, flip_second = kind % 2, kind // 2
            fy, fx = (flip_first, flip_second) if a == 0 else (flip_second, flip_first)
            return slot(out, zz, 1 - y if fy else y, 1 - x if fx else x, c)

        arrays.append((a, src, out, first, second, at))

    def wait(a, at, step, kind, sem):
        here = at(step, kind)
        pltpu.make_async_remote_copy(
            src_ref=here, dst_ref=here, send_sem=own_sem.at[a], recv_sem=sem,
            device_id=c_peer, device_id_type=MESH,
        ).wait_recv()

    for a, src, out, first, second, at in arrays:
        here = slot(out, z, y, x, c)
        for s in range(1, line):
            push(src, here, (2 * lax.rem(z + s, line) + y, h), send_sem.at[a, s - 1], z_sem.at[a, s])
        own = pltpu.make_async_copy(src, here, own_sem.at[a])
        own.start()
        owns.append(own)
    for s in range(1, groups):
        here = w_ref.at[pl.ds(pl.multiple_of(e * rows, rows), rows), :]
        push(tab_ref, here, ring[s - 1], tab_send.at[s], tab_recv.at[s])
    own = pltpu.make_async_copy(
        tab_ref, w_ref.at[pl.ds(pl.multiple_of(e * rows, rows), rows), :], own_sem.at[2]
    )
    own.start()
    owns.append(own)

    base = line - 1
    for s in range(line + 2):
        for a, src, out, first, second, at in arrays:
            if s < line:
                if s > 0:
                    wait(a, at, s, 0, z_sem.at[a, s])
                there = at(s, 0)
                have = src if s == 0 else there
                push(have, there, first, send_sem.at[a, base + s], p_sem.at[a, s])
                push(have, there, second, send_sem.at[a, base + line + s], q_sem.at[a, s])
                push(have, there, c_peer, send_sem.at[a, base + 3 * line + s], c_sem.at[a, s])
            if 1 <= s <= line:
                j = s - 1
                wait(a, at, j, 1, p_sem.at[a, j])
                there = at(j, 1)
                push(there, there, second, send_sem.at[a, base + 2 * line + j], q_sem.at[a, line + j])
                push(there, there, c_peer, send_sem.at[a, base + 4 * line + j], c_sem.at[a, line + j])
                wait(a, at, j, 2, q_sem.at[a, j])
                there = at(j, 2)
                push(there, there, c_peer, send_sem.at[a, base + 5 * line + j], c_sem.at[a, 2 * line + j])
            if s >= 2:
                j = s - 2
                wait(a, at, j, 3, q_sem.at[a, line + j])
                there = at(j, 3)
                push(there, there, c_peer, send_sem.at[a, base + 6 * line + j], c_sem.at[a, 3 * line + j])
    for s in range(1, groups):
        peer = lax.rem(e - s + groups, groups)
        here = w_ref.at[pl.ds(pl.multiple_of(peer * rows, rows), rows), :]
        pltpu.make_async_remote_copy(
            src_ref=here, dst_ref=here, send_sem=tab_send.at[s], recv_sem=tab_recv.at[s],
            device_id=c_peer, device_id_type=MESH,
        ).wait_recv()
    for a, src, out, first, second, at in arrays:
        for kind in range(4):
            for j in range(line):
                flips = (kind % 2, kind // 2) if a == 0 else (kind // 2, kind % 2)
                here = slot(
                    out, lax.rem(z - j + line, line),
                    1 - y if flips[0] else y, 1 - x if flips[1] else x, 1 - c,
                )
                pltpu.make_async_remote_copy(
                    src_ref=here, dst_ref=here, send_sem=own_sem.at[a],
                    recv_sem=c_sem.at[a, kind * line + j], device_id=c_peer, device_id_type=MESH,
                ).wait_recv()
    for own in owns:
        own.wait()
    for copy in sends:
        copy.wait_send()


def gather_fast(tokens, cotangent, table, groups, halves):
    rows, quarter = tokens.shape
    line = groups // 2
    padded = jnp.pad(table, ((0, 0), (0, -table.shape[1] % LANES)))
    full = jax.ShapeDtypeStruct((groups * rows, halves * quarter), tokens.dtype)
    dma = pltpu.SemaphoreType.DMA
    return pl.pallas_call(
        functools.partial(gather_kernel, groups),
        out_shape=(full, full, jax.ShapeDtypeStruct((groups * rows, padded.shape[1]), table.dtype)),
        in_specs=[pl.BlockSpec(memory_space=pltpu.VMEM)] * 3,
        out_specs=[pl.BlockSpec(memory_space=pl.ANY)] * 3,
        scratch_shapes=[
            dma((2, 8 * line)), dma((2, line)), dma((2, line)), dma((2, 2 * line)),
            dma((2, 4 * line)), dma((groups,)), dma((groups,)), dma((3,)),
        ],
        compiler_params=pltpu.CompilerParams(collective_id=0, has_side_effects=True),
    )(tokens, cotangent, padded)


def scatter_kernel(
    groups, part, out_ref, core, one_a, one_b, two_a, two_b, last, send_sem, recv_sem,
):
    line = groups // 2
    z, y, x, c = place(groups)
    e, h = 2 * z + y, 2 * x + c
    wide = out_ref.shape[1] // 2
    f32 = jnp.float32
    y_peer = (2 * z + 1 - y, h)
    x_peer = (e, 2 * (1 - x) + c)
    c_peer = (e, 2 * x + 1 - c)
    others = [(2 * lax.rem(z + s, line) + y, h) for s in range(1, line)]
    greet(others + [y_peer, x_peer, c_peer])

    def col(xx, cc, side):
        return pl.ds(pl.multiple_of((2 * xx + cc) * 2 * wide + side * wide, wide), wide)

    def push(src, dst, peer, number):
        copy = pltpu.make_async_remote_copy(
            src_ref=src, dst_ref=dst, send_sem=send_sem.at[number], recv_sem=recv_sem.at[number],
            device_id=peer, device_id_type=MESH,
        )
        copy.start()
        return copy

    def add(dst, src):
        dst[...] = (dst[...].astype(f32) + src[...].astype(f32)).astype(dst.dtype)

    copies = []
    order = ((0, 0), (1, 0), (1, 1), (0, 1))
    for number, (side, keep) in enumerate(order):
        xx = x if keep else 1 - x
        copies.append(
            push(part.at[:, :, :, col(xx, 1 - c, side)], core.at[side, keep], c_peer, number)
        )

    def settle(number):
        side, keep = order[number]
        copies[number].wait_recv()
        xx = x if keep else 1 - x

        @pl.loop(0, line)
        def _(i):
            for j in range(2):
                add(core.at[side, keep, i, j], part.at[i, j, :, col(xx, c, side)])

    settle(0)
    a1 = push(core.at[0, 0], one_a, x_peer, 4)
    settle(1)
    settle(2)
    b1 = push(core.at[1, :, :, 1 - y], one_b, y_peer, 5)
    settle(3)
    a1.wait_recv()

    @pl.loop(0, line)
    def _(i):
        for j in range(2):
            add(one_a.at[i, j], core.at[0, 1, i, j])

    a2 = push(one_a.at[:, 1 - y], two_a, y_peer, 6)
    b1.wait_recv()

    @pl.loop(0, line)
    def _(i):
        for j in range(2):
            add(one_b.at[j, i], core.at[1, j, i, y])

    b2 = push(one_b.at[0], two_b, x_peer, 7)
    copies += [a1, b1, a2, b2]
    tails = ([], [])
    for side, copy, two in ((0, a2, two_a), (1, b2, two_b)):
        copy.wait_recv()

        @pl.loop(0, line)
        def _(i):
            add(two.at[i], one_a.at[i, y] if side == 0 else one_b.at[1, i])

        for s in range(1, line):
            number = 8 + side * line + s
            tails[side].append(
                push(two.at[lax.rem(z + s, line)], last.at[side, s - 1], others[s - 1], number)
            )
    for side, two in ((0, two_a), (1, two_b)):
        total = two[z].astype(f32)
        for s, copy in enumerate(tails[side]):
            copy.wait_recv()
            total = total + last[side, s].astype(f32)
        out_ref[:, side * wide:(side + 1) * wide] = total.astype(out_ref.dtype)
    for copy in copies + tails[0] + tails[1]:
        copy.wait_send()


def scatter_fast(part, groups, halves, rows, quarter):
    line = groups // 2
    wide = quarter // 2
    b16 = part.dtype
    dma = pltpu.SemaphoreType.DMA
    return pl.pallas_call(
        functools.partial(scatter_kernel, groups),
        out_shape=jax.ShapeDtypeStruct((rows, quarter), b16),
        in_specs=[pl.BlockSpec(memory_space=pltpu.VMEM)],
        out_specs=pl.BlockSpec(memory_space=pltpu.VMEM),
        scratch_shapes=[
            pltpu.VMEM((2, 2, line, 2, rows, wide), b16),
            pltpu.VMEM((line, 2, rows, wide), b16),
            pltpu.VMEM((2, line, rows, wide), b16),
            pltpu.VMEM((line, rows, wide), b16),
            pltpu.VMEM((line, rows, wide), b16),
            pltpu.VMEM((2, line - 1, rows, wide), b16),
            dma((8 + 2 * line,)),
            dma((8 + 2 * line,)),
        ],
        compiler_params=pltpu.CompilerParams(collective_id=1, has_side_effects=True),
    )(part.reshape(line, 2, rows, halves * quarter))


def per_device(tokens, cotangent, route, prob, w_gate, w_up, w_down):
    tok_rows, quarter = tokens.shape
    local_exp, units, width = w_gate.shape
    groups = lax.axis_size("expert")
    halves = lax.axis_size("half")
    experts = local_exp * groups
    total = groups * tok_rows
    f32 = jnp.float32
    me = lax.axis_index("expert")

    hit = route[:, :, None] == jnp.arange(experts, dtype=route.dtype)
    table = jnp.sum(jnp.where(hit, prob[:, :, None], 0).astype(f32), axis=1).astype(prob.dtype)
    fast = (
        groups > 2 and groups % 2 == 0 and halves == 2 * 2
        and tok_rows % 16 == 0 and quarter % (2 * LANES) == 0
        and total * width * 2 <= (1 << 23)
    )
    if fast:
        x, d, mine = gather_fast(tokens, cotangent, table, groups, halves)
        mine = lax.dynamic_slice_in_dim(mine, me * local_exp, local_exp, axis=1)
    else:
        mine = lax.all_to_all(
            table.reshape(tok_rows, groups, local_exp), "expert",
            split_axis=1, concat_axis=0, tiled=True,
        ).reshape(total, local_exp)
        x = gather_all(tokens, groups, halves)
        d = gather_all(cotangent, groups, halves)
    weight = jnp.repeat(mine.astype(f32), units, axis=1)

    wg = w_gate.reshape(local_exp * units, width)
    wu = w_up.reshape(local_exp * units, width)
    wd = w_down.reshape(local_exp * units, width)
    nt = (((1,), (1,)), ((), ()))
    tn = (((0,), (0,)), ((), ()))
    gate = lax.dot_general(x, wg, nt, preferred_element_type=f32)
    upval = lax.dot_general(x, wu, nt, preferred_element_type=f32)
    raw = lax.dot_general(d, wd, nt, preferred_element_type=f32)
    sig = jax.nn.sigmoid(gate)
    act = gate * sig
    hidden = act * upval
    score = jnp.sum((hidden * raw).reshape(total, local_exp, units), axis=2)
    dact = weight * raw
    hp = (weight * hidden).astype(jnp.bfloat16)
    dgate = (dact * upval * sig * (1.0 + gate * (1.0 - sig))).astype(jnp.bfloat16)
    dup = (dact * act).astype(jnp.bfloat16)
    part = lax.dot_general(
        jnp.concatenate([dgate, dup], axis=1), jnp.concatenate([wg, wu], axis=0),
        (((1,), (0,)), ((), ())), preferred_element_type=f32,
    ).astype(jnp.bfloat16)
    if fast:
        grad_tokens = scatter_fast(part, groups, halves, tok_rows, quarter)
    else:
        part = part.reshape(groups, tok_rows, halves, quarter).transpose(0, 2, 1, 3)
        grad_tokens = lax.psum_scatter(
            part.reshape(groups * halves * tok_rows, quarter), BOTH,
            scatter_dimension=0, tiled=True,
        )
    sent = jnp.broadcast_to(
        score.reshape(groups, 1, tok_rows, local_exp), (groups, halves, tok_rows, local_exp)
    ).reshape(groups * halves, tok_rows * local_exp)
    back = lax.all_to_all(sent, BOTH, split_axis=0, concat_axis=0, tiled=True)
    back = jnp.sum(back.reshape(groups, halves, tok_rows, local_exp), axis=1)
    back = back.transpose(1, 0, 2).reshape(tok_rows, 1, experts)
    grad_prob = jnp.sum(jnp.where(hit, back, 0), axis=2)
    shape = (local_exp, units, width)
    grad_gate = lax.dot_general(dgate, x, tn, preferred_element_type=f32).astype(jnp.bfloat16)
    grad_up = lax.dot_general(dup, x, tn, preferred_element_type=f32).astype(jnp.bfloat16)
    grad_down = lax.dot_general(hp, d, tn, preferred_element_type=f32).astype(jnp.bfloat16)
    return (
        grad_tokens,
        grad_prob,
        grad_gate.reshape(shape),
        grad_up.reshape(shape),
        grad_down.reshape(shape),
    )


def solution(mesh):
    in_specs = (
        P("expert", "half"),
        P("expert", "half"),
        P("expert", None),
        P("expert", None),
        P("expert", "half", None),
        P("expert", "half", None),
        P("expert", "half", None),
    )
    out_specs = (
        P("expert", "half"),
        P("expert", None),
        P("expert", "half", None),
        P("expert", "half", None),
        P("expert", "half", None),
    )
    return jax.shard_map(
        per_device, mesh=mesh, in_specs=in_specs, out_specs=out_specs, check_vma=False
    )
```

time: 396 us -> 137 us (0.35)
  blocking collectives: 123 us -> 0 us
  waiting for transfers between devices: 113 us -> 0.01 us
  Pallas kernels: 0 us -> 92.7 us
  local copies, waits for them, and re-layouts: 61.2 us -> 3.95 us
  matrix products: 55.6 us -> 26.8 us
  other arithmetic: 17.2 us -> 3.1 us
  between operations: 14 us -> 0.84 us
    all_to_all x3 -> x0, blocking collectives: 117 us -> none  [the longest x1 55.4 us: per_device(): lax.all_to_all(pack(tokens), 'expert', split_axis=0, concat_axis=0, tiled...]
    pallas_call x0 -> x2, Pallas kernels: none -> 92.7 us  [the longest x1 51.6 us: gather_fast(): pl.pallas_call(functools.partial(gather_kernel, groups), out_shape=(full,...]
    reduce_scatter x1 -> x0, waiting for transfers between devices: 58.4 us -> none  [per_device(): lax.psum_scatter(part.astype(jnp.float32).astype(jnp.bfloat16), 'half', s...]
    gather x5 -> x0, local copies, waits for them, and re-layouts: 45.2 us -> none  [the longest x2 18.3 us: pack(): rows[token_of]]
    all_gather x2 -> x0, waiting for transfers between devices: 29.7 us -> none  [the longest x1 29.7 us: per_device(): lax.all_gather(sent_d, 'half', axis=2, tiled=True)]
    dot_general x8 -> x7, matrix products: 55.6 us -> 26.8 us  [the longest x1 5.27 us: per_device(): lax.dot_general(dgate, x, tn, preferred_element_type=f32)]
    all_to_all x2 -> x1, waiting for transfers between devices: 24.9 us -> 0.01 us  [per_device(): back = lax.all_to_all(sent, BOTH, split_axis=0, concat_axis=0, tiled=True)]
    scatter x2 -> x0, local copies, waits for them, and re-layouts: 8.66 us -> none  [the longest x1 4.34 us: per_device(): filled = jnp.zeros((slots,), jnp.bool_).at[slot_of].set(True)]
  transfers between devices with their start and end apart: 5 -> 1, of which waited for: 3 -> 0; matrix products, arithmetic and copies ran while one was open for 13% -> 12% of each run, Pallas kernels for 0% -> 30%
where the time goes in v1:
time: 137 us
  Pallas kernels  92.7 us (68%)
  matrix products  26.8 us (20%)
  starting transfers between devices  9.59 us (7%)
  local copies, waits for them, and re-layouts  3.95 us (3%)
  other arithmetic  3.1 us (2%)
    pallas_call x1, Pallas kernels, gather_fast(): pl.pallas_call(functools.partial(gather_kernel, groups), out_shape=(full,...  51.6 us
    pallas_call x1, Pallas kernels, scatter_fast(): pl.pallas_call(functools.partial(scatter_kernel, groups), out_shape=jax.S...  41.1 us
    all_to_all x1, starting transfers between devices, per_device(): back = lax.all_to_all(sent, BOTH, split_axis=0, concat_axis=0, tiled=True)  9.59 us
    dot_general x1, matrix products, per_device(): lax.dot_general(dgate, x, tn, preferred_element_type=f32)  5.27 us
    dot_general x1, matrix products, per_device(): lax.dot_general(jnp.concatenate([dgate, dup], axis=1), jnp.concatenate([w...  5.12 us
    dot_general x1, matrix products, per_device(): gate = lax.dot_general(x, wg, nt, preferred_element_type=f32)  4.65 us
    dot_general x1, matrix products, per_device(): raw = lax.dot_general(d, wd, nt, preferred_element_type=f32)  3.95 us
    dot_general x1, matrix products, per_device(): lax.dot_general(dup, x, tn, preferred_element_type=f32).astype(jnp.bfloat16)  2.97 us
  transfers between devices with their start and end apart: 1, of which 0 were waited for; matrix products, arithmetic and copies ran while one was open for 12% of the time, Pallas kernels for 30%

profile of v1, /device:TPU:0, one launch (start us, length us, event | category | flops | bytes accessed | tf_op | source)
XLA Modules:
  0.0 137.0 jit_solution(43676077150619855)
XLA Ops:
  0.7 0.8 fusion.9
  1.5 0.1 copy.38
  1.6 0.6 pad.4.tab_ref
  2.2 51.6 %shard_map.110 = (bf16[1024,2048]{1,0:T(8,128)(2,1)}, bf16[1024,2048]{1,0:T(8,128)(2,1)}, bf16[1024,128]{1,0:T(8,128)(2,1)}) custom-call(bf16[128,512]{1,0:T(8,128)(2,1)} %tok_ref.1, bf16[128,512]{1,0:T(8,128)(2,1)} %cot_ref.1, bf16[128,128]{1,0:T(8,128)(2,1)} %pad.4.tab_ref), custom_call_target="tpu_custom_call" | custom-call | tf_op jit(solution)/shard_map/pallas_call | solution.py:155
  53.9 1.1 dynamic-slice_convert_fusion
  55.0 0.2 copy.39
  55.2 4.7 %fusion.12 = f32[1024,384]{0,1:T(8,128)S(1)} fusion(bf16[1024,2048]{1,0:T(8,128)(2,1)} %get-tuple-element.10, bf16[384,2048]{1,0:T(8,128)(2,1)} %bitcast.52), kind=kOutput, calls=%fused_computation.26 | convolution fusion | flops 1610612736 | bytes 7340032 | tf_op jit(solution)/shard_map/dot_general | solution.py:318
  59.9 1.8 %fusion.11 = f32[1024,384]{0,1:T(8,128)S(1)} fusion(bf16[1024,2048]{1,0:T(8,128)(2,1)S(1)} %copy-done.8, bf16[384,2048]{1,0:T(8,128)(2,1)S(1)} %bitcast.50), kind=kOutput, calls=%fused_computation.25 | convolution fusion | flops 1610612736 | bytes 7340032 | tf_op jit(solution)/shard_map/dot_general | solution.py:319
  61.7 0.3 copy-done.1
  62.0 3.9 %multiply_multiply_fusion = (f32[1024,384]{0,1:T(8,128)S(1)}, bf16[1024,384]{0,1:T(8,128)(2,1)}, bf16[1024,384]{0,1:T(8,128)(2,1)}, bf16[1024,384]{0,1:T(8,128)(2,1)}) fusion(f32[1024,384]{0,1:T(8,128)S(1)} %fusion.11, f32[1024,384]{0,1:T(8,128)S(1)} %fusion.12, f32[1024,2]{0,1:T(2,128)S(1)} %copy.39, bf16[1024,2048]{1,0:T(8,128)(2,1)S(1)} %copy-done.1, ...), kind=kOutput, calls=%fused_computation.17 | convolution fusion | flops 1617690624 | bytes 12853248 | tf_op jit(solution)/shard_map/dot_general | solution.py:320
  66.1 0.1 copy.40
  66.3 0.3 broadcast_in_dim.43
  66.6 0.3 all_to_all.6
  66.9 0.7 copy.41
  67.6 9.6 %all-to-all-start = ((f32[32,1,256]{2,1,0:T(1,128)}), f32[32,1,256]{2,1,0:T(1,128)S(1)}, u32[]{:S(2)}, u32[]{:S(2)}) async-start(f32[32,1,256]{2,1,0:T(1,128)} %copy.41), calls=%async_computation | async-start | bytes 65536 | tf_op jit(solution)/shard_map/all_to_all | solution.py:344
  77.2 5.3 %convolution_convert_fusion.3 = bf16[384,2048]{1,0:T(8,128)(2,1)} fusion(bf16[1024,384]{0,1:T(8,128)(2,1)S(1)} %copy-done.4, bf16[1024,2048]{1,0:T(8,128)(2,1)} %get-tuple-element.10), kind=kOutput, calls=%fused_computation.6 | convolution fusion | flops 1611399168 | bytes 6553600 | tf_op jit(solution)/shard_map/dot_general | solution.py:349
  82.5 3.0 %convolution_convert_fusion.2 = bf16[384,2048]{1,0:T(8,128)(2,1)} fusion(bf16[1024,384]{0,1:T(8,128)(2,1)S(1)} %copy-done.5, bf16[1024,2048]{1,0:T(8,128)(2,1)S(1)} %copy-done.9), kind=kOutput, calls=%fused_computation.5 | convolution fusion | flops 1611399168 | bytes 6553600 | tf_op jit(solution)/shard_map/dot_general | solution.py:350
  85.5 5.1 %convolution_convert_fusion = bf16[1024,2048]{1,0:T(8,128)(2,1)} fusion(bf16[384,2048]{1,0:T(8,128)(2,1)S(1)} %bitcast.51, bf16[384,2048]{1,0:T(8,128)(2,1)S(1)} %bitcast.53, bf16[1024,384]{0,1:T(8,128)(2,1)S(1)} %copy-done.5, bf16[1024,384]{0,1:T(8,128)(2,1)S(1)} %copy-done.4), kind=kOutput, calls=%fused_computation | convolution fusion | flops 3232759808 | bytes 8912896 | tf_op jit(solution)/shard_map/dot_general | solution.py:329
  90.6 3.0 %convolution_convert_fusion.1 = bf16[384,2048]{1,0:T(8,128)(2,1)} fusion(bf16[1024,384]{0,1:T(8,128)(2,1)S(1)} %copy-done.3, bf16[1024,2048]{1,0:T(8,128)(2,1)S(1)} %copy-done.2), kind=kOutput, calls=%fused_computation.4 | convolution fusion | flops 1611399168 | bytes 6553600 | tf_op jit(solution)/shard_map/dot_general | solution.py:351
  93.6 41.1 %shard_map.111 = bf16[128,512]{1,0:T(8,128)(2,1)} custom-call(bf16[4,2,128,2048]{3,2,1,0:T(8,128)(2,1)} %bitcast.45), custom_call_target="tpu_custom_call" | custom-call | tf_op jit(solution)/shard_map/pallas_call | solution.py:265
  134.8 0.3 reshape.57
  135.1 0.4 reduce_sum.41
  135.7 0.6 select_reduce_fusion
  136.3 0.7 copy.48
  (30 shorter events, 0.3 us)
Async XLA Ops:
  0.6 61.1 %copy-start = (bf16[2,192,2048]{2,1,0:T(8,128)(2,1)S(1)}, bf16[2,192,2048]{2,1,0:T(8,128)(2,1)}, u32[]{:S(2)}) copy-start(bf16[2,192,2048]{2,1,0:T(8,128)(2,1)} %param.13) | copy-start | bytes 4718596
  55.2 4.7 %copy-start.8 = (bf16[1024,2048]{1,0:T(8,128)(2,1)S(1)}, bf16[1024,2048]{1,0:T(8,128)(2,1)}, u32[]{:S(2)}) copy-start(bf16[1024,2048]{1,0:T(8,128)(2,1)} %get-tuple-element.10) | copy-start | bytes 12582916
  55.2 4.7 %copy-start.10 = (bf16[2,192,2048]{2,1,0:T(8,128)(2,1)S(1)}, bf16[2,192,2048]{2,1,0:T(8,128)(2,1)}, u32[]{:S(2)}) copy-start(bf16[2,192,2048]{2,1,0:T(8,128)(2,1)} %param.12) | copy-start | bytes 4718596
  59.8 2.2 %copy-start.1 = (bf16[1024,2048]{1,0:T(8,128)(2,1)S(1)}, bf16[1024,2048]{1,0:T(8,128)(2,1)}, u32[]{:S(2)}) copy-start(bf16[1024,2048]{1,0:T(8,128)(2,1)} %get-tuple-element.9) | copy-start | bytes 12582916
  66.1 11.1 %copy-start.4 = (bf16[1024,384]{0,1:T(8,128)(2,1)S(1)}, bf16[1024,384]{0,1:T(8,128)(2,1)}, u32[]{:S(2)}) copy-start(bf16[1024,384]{0,1:T(8,128)(2,1)} %get-tuple-element.12) | copy-start | bytes 2359300
  67.6 67.1 %all-to-all-start = ((f32[32,1,256]{2,1,0:T(1,128)}), f32[32,1,256]{2,1,0:T(1,128)S(1)}, u32[]{:S(2)}, u32[]{:S(2)}) async-start(f32[32,1,256]{2,1,0:T(1,128)} %copy.41), calls=%async_computation | async-start | bytes 65536 | tf_op jit(solution)/shard_map/all_to_all | solution.py:344
  77.2 5.3 %copy-start.5 = (bf16[1024,384]{0,1:T(8,128)(2,1)S(1)}, bf16[1024,384]{0,1:T(8,128)(2,1)}, u32[]{:S(2)}) copy-start(bf16[1024,384]{0,1:T(8,128)(2,1)} %get-tuple-element.14) | copy-start | bytes 2359300
  77.2 5.3 %copy-start.9 = (bf16[1024,2048]{1,0:T(8,128)(2,1)S(1)}, bf16[1024,2048]{1,0:T(8,128)(2,1)}, u32[]{:S(2)}) copy-start(bf16[1024,2048]{1,0:T(8,128)(2,1)} %get-tuple-element.10) | copy-start | bytes 12582916
  82.5 3.0 %copy-start.11 = (bf16[2,192,2048]{2,1,0:T(8,128)(2,1)S(1)}, bf16[2,192,2048]{2,1,0:T(8,128)(2,1)}, u32[]{:S(2)}) copy-start(bf16[2,192,2048]{2,1,0:T(8,128)(2,1)} %param.12) | copy-start | bytes 4718596
  82.5 3.0 %copy-start.12 = (bf16[2,192,2048]{2,1,0:T(8,128)(2,1)S(1)}, bf16[2,192,2048]{2,1,0:T(8,128)(2,1)}, u32[]{:S(2)}) copy-start(bf16[2,192,2048]{2,1,0:T(8,128)(2,1)} %param.11) | copy-start | bytes 4718596
  85.5 5.1 %copy-start.2 = (bf16[1024,2048]{1,0:T(8,128)(2,1)S(1)}, bf16[1024,2048]{1,0:T(8,128)(2,1)}, u32[]{:S(2)}) copy-start(bf16[1024,2048]{1,0:T(8,128)(2,1)} %get-tuple-element.9) | copy-start | bytes 12582916
  85.5 5.1 %copy-start.3 = (bf16[1024,384]{0,1:T(8,128)(2,1)S(1)}, bf16[1024,384]{0,1:T(8,128)(2,1)}, u32[]{:S(2)}) copy-start(bf16[1024,384]{0,1:T(8,128)(2,1)} %get-tuple-element.13) | copy-start | bytes 2359300
  134.7 1.0 copy-start.7
  134.7 1.6 %copy-start.6 = (bf16[128,512]{1,0:T(8,128)(2,1)S(1)}, bf16[128,512]{1,0:T(8,128)(2,1)}, u32[]{:S(2)}) copy-start(bf16[128,512]{1,0:T(8,128)(2,1)} %shard_map.111) | copy-start | bytes 393220

commit v2 on v1

--- a/solution.py
+++ b/solution.py
@@ -23,6 +23,15 @@
 def place(groups):
     e, h = lax.axis_index("expert"), lax.axis_index("half")
     return lax.div(e, 2), lax.rem(e, 2), lax.div(h, 2), lax.rem(h, 2)
+
+
+def across(z, step):
+    bit = 1
+    while bit <= step:
+        if step & bit:
+            z = z + bit * (1 - 2 * lax.rem(lax.div(z, bit), 2))
+        bit *= 2
+    return z
 
 
 def greet(peers):
@@ -66,7 +75,7 @@
         first, second = (y_peer, x_peer) if a == 0 else (x_peer, y_peer)
 
         def at(step, kind, out=out, a=a):
-            zz = lax.rem(z - step + line, line)
+            zz = across(z, step)
             flip_first, flip_second = kind % 2, kind // 2
             fy, fx = (flip_first, flip_second) if a == 0 else (flip_second, flip_first)
             return slot(out, zz, 1 - y if fy else y, 1 - x if fx else x, c)
@@ -83,7 +92,7 @@
     for a, src, out, first, second, at in arrays:
         here = slot(out, z, y, x, c)
         for s in range(1, line):
-            push(src, here, (2 * lax.rem(z + s, line) + y, h), send_sem.at[a, s - 1], z_sem.at[a, s])
+            push(src, here, (2 * across(z, s) + y, h), send_sem.at[a, s - 1], z_sem.at[a, s])
         own = pltpu.make_async_copy(src, here, own_sem.at[a])
         own.start()
         owns.append(own)
@@ -133,7 +142,7 @@
             for j in range(line):
                 flips = (kind % 2, kind // 2) if a == 0 else (kind // 2, kind % 2)
                 here = slot(
-                    out, lax.rem(z - j + line, line),
+                    out, across(z, j),
                     1 - y if flips[0] else y, 1 - x if flips[1] else x, 1 - c,
                 )
                 pltpu.make_async_remote_copy(
@@ -166,7 +175,8 @@
 
 
 def scatter_kernel(
-    groups, part, out_ref, core, one_a, one_b, two_a, two_b, last, send_sem, recv_sem,
+    groups, halves, part, score, out_ref, back_ref, core, one_a, one_b, two_a, two_b, last,
+    send_sem, recv_sem, score_send, score_recv, own_sem,
 ):
     line = groups // 2
     z, y, x, c = place(groups)
@@ -177,7 +187,11 @@
     x_peer = (e, 2 * (1 - x) + c)
     c_peer = (e, 2 * x + 1 - c)
     others = [(2 * lax.rem(z + s, line) + y, h) for s in range(1, line)]
-    greet(others + [y_peer, x_peer, c_peer])
+    peers = [
+        (lax.rem(e + i, groups), lax.rem(h + j, halves))
+        for i in range(groups) for j in range(halves) if i + j
+    ]
+    greet(peers)
 
     def col(xx, cc, side):
         return pl.ds(pl.multiple_of((2 * xx + cc) * 2 * wide + side * wide, wide), wide)
@@ -195,6 +209,21 @@
 
     copies = []
     order = ((0, 0), (1, 0), (1, 1), (0, 1))
+    scores = []
+    mine = e * halves + h
+
+    def send_scores():
+        for number, peer in enumerate(peers):
+            copy = pltpu.make_async_remote_copy(
+                src_ref=score.at[peer[0]], dst_ref=back_ref.at[mine],
+                send_sem=score_send.at[number], recv_sem=score_recv.at[number],
+                device_id=peer, device_id_type=MESH,
+            )
+            copy.start()
+            scores.append(copy)
+
+    own = pltpu.make_async_copy(score.at[e], back_ref.at[mine], own_sem.at[0])
+    own.start()
     for number, (side, keep) in enumerate(order):
         xx = x if keep else 1 - x
         copies.append(
@@ -216,6 +245,7 @@
     settle(1)
     settle(2)
     b1 = push(core.at[1, :, :, 1 - y], one_b, y_peer, 5)
+    send_scores()
     settle(3)
     a1.wait_recv()
 
@@ -253,20 +283,26 @@
             copy.wait_recv()
             total = total + last[side, s].astype(f32)
         out_ref[:, side * wide:(side + 1) * wide] = total.astype(out_ref.dtype)
-    for copy in copies + tails[0] + tails[1]:
+    for copy in scores:
+        copy.wait_recv()
+    own.wait()
+    for copy in copies + tails[0] + tails[1] + scores:
         copy.wait_send()
 
 
-def scatter_fast(part, groups, halves, rows, quarter):
+def scatter_fast(part, score, groups, halves, rows, quarter):
     line = groups // 2
     wide = quarter // 2
     b16 = part.dtype
     dma = pltpu.SemaphoreType.DMA
     return pl.pallas_call(
-        functools.partial(scatter_kernel, groups),
-        out_shape=jax.ShapeDtypeStruct((rows, quarter), b16),
-        in_specs=[pl.BlockSpec(memory_space=pltpu.VMEM)],
-        out_specs=pl.BlockSpec(memory_space=pltpu.VMEM),
+        functools.partial(scatter_kernel, groups, halves),
+        out_shape=(
+            jax.ShapeDtypeStruct((rows, quarter), b16),
+            jax.ShapeDtypeStruct((groups * halves,) + score.shape[1:], score.dtype),
+        ),
+        in_specs=[pl.BlockSpec(memory_space=pltpu.VMEM)] * 2,
+        out_specs=[pl.BlockSpec(memory_space=pltpu.VMEM)] * 2,
         scratch_shapes=[
             pltpu.VMEM((2, 2, line, 2, rows, wide), b16),
             pltpu.VMEM((line, 2, rows, wide), b16),
@@ -276,9 +312,12 @@
             pltpu.VMEM((2, line - 1, rows, wide), b16),
             dma((8 + 2 * line,)),
             dma((8 + 2 * line,)),
+            dma((groups * halves - 1,)),
+            dma((groups * halves - 1,)),
+            dma((1,)),
         ],
         compiler_params=pltpu.CompilerParams(collective_id=1, has_side_effects=True),
-    )(part.reshape(line, 2, rows, halves * quarter))
+    )(part.reshape(line, 2, rows, halves * quarter), score)
 
 
 def per_device(tokens, cotangent, route, prob, w_gate, w_up, w_down):
@@ -294,8 +333,8 @@
     hit = route[:, :, None] == jnp.arange(experts, dtype=route.dtype)
     table = jnp.sum(jnp.where(hit, prob[:, :, None], 0).astype(f32), axis=1).astype(prob.dtype)
     fast = (
-        groups > 2 and groups % 2 == 0 and halves == 2 * 2
-        and tok_rows % 16 == 0 and quarter % (2 * LANES) == 0
+        groups > 2 and groups & (groups - 1) == 0 and halves == 2 * 2
+        and tok_rows % LANES == 0 and quarter % (2 * LANES) == 0
         and total * width * 2 <= (1 << 23)
     )
     if fast:
@@ -331,19 +370,23 @@
         (((1,), (0,)), ((), ())), preferred_element_type=f32,
     ).astype(jnp.bfloat16)
     if fast:
-        grad_tokens = scatter_fast(part, groups, halves, tok_rows, quarter)
+        by_group = score.reshape(groups, tok_rows, local_exp).transpose(0, 2, 1)
+        by_group = jnp.pad(by_group, ((0, 0), (0, -local_exp % 8), (0, 0)))
+        grad_tokens, back = scatter_fast(part, by_group, groups, halves, tok_rows, quarter)
+        back = back[:, :local_exp].reshape(groups, halves, local_exp, tok_rows)
+        back = jnp.sum(back, axis=1).transpose(2, 0, 1).reshape(tok_rows, 1, experts)
     else:
         part = part.reshape(groups, tok_rows, halves, quarter).transpose(0, 2, 1, 3)
         grad_tokens = lax.psum_scatter(
             part.reshape(groups * halves * tok_rows, quarter), BOTH,
             scatter_dimension=0, tiled=True,
         )
-    sent = jnp.broadcast_to(
-        score.reshape(groups, 1, tok_rows, local_exp), (groups, halves, tok_rows, local_exp)
-    ).reshape(groups * halves, tok_rows * local_exp)
-    back = lax.all_to_all(sent, BOTH, split_axis=0, concat_axis=0, tiled=True)
-    back = jnp.sum(back.reshape(groups, halves, tok_rows, local_exp), axis=1)
-    back = back.transpose(1, 0, 2).reshape(tok_rows, 1, experts)
+        sent = jnp.broadcast_to(
+            score.reshape(groups, 1, tok_rows, local_exp), (groups, halves, tok_rows, local_exp)
+        ).reshape(groups * halves, tok_rows * local_exp)
+        back = lax.all_to_all(sent, BOTH, split_axis=0, concat_axis=0, tiled=True)
+        back = jnp.sum(back.reshape(groups, halves, tok_rows, local_exp), axis=1)
+        back = back.transpose(1, 0, 2).reshape(tok_rows, 1, experts)
     grad_prob = jnp.sum(jnp.where(hit, back, 0), axis=2)
     shape = (local_exp, units, width)
     grad_gate = lax.dot_general(dgate, x, tn, preferred_element_type=f32).astype(jnp.bfloat16)

time: 137 us -> 131 us (0.956)
  starting transfers between devices: 9.59 us -> 0 us
  Pallas kernels: 92.7 us -> 94.6 us
    all_to_all x1 -> x0, starting transfers between devices: 9.59 us -> none  [per_device(): back = lax.all_to_all(sent, BOTH, split_axis=0, concat_axis=0, tiled=True)]
    unnamed x28 -> x21, local copies, waits for them, and re-layouts: 1.05 us -> 3.35 us
    pallas_call x1, Pallas kernels: 41.1 us -> 43 us  [scatter_fast(): pl.pallas_call(functools.partial(scatter_kernel, groups, halves), out_sha...]
  transfers between devices with their start and end apart: 1 -> 0, of which waited for: 0 -> 0; matrix products, arithmetic and copies ran while one was open for 12% -> 0% of each run, Pallas kernels for 30% -> 0%
where the time goes in v2:
time: 131 us
  Pallas kernels  94.6 us (72%)
  matrix products  26.9 us (21%)
  local copies, waits for them, and re-layouts  4.9 us (4%)
  other arithmetic  3.44 us (3%)
    pallas_call x1, Pallas kernels, gather_fast(): pl.pallas_call(functools.partial(gather_kernel, groups), out_shape=(full,...  51.6 us
    pallas_call x1, Pallas kernels, scatter_fast(): pl.pallas_call(functools.partial(scatter_kernel, groups, halves), out_sha...  43 us
    dot_general x1, matrix products, per_device(): lax.dot_general(dgate, x, tn, preferred_element_type=f32)  5.51 us
    dot_general x1, matrix products, per_device(): lax.dot_general(jnp.concatenate([dgate, dup], axis=1), jnp.concatenate([w...  5.27 us
    dot_general x1, matrix products, per_device(): gate = lax.dot_general(x, wg, nt, preferred_element_type=f32)  4.65 us
    dot_general x1, matrix products, per_device(): raw = lax.dot_general(d, wd, nt, preferred_element_type=f32)  3.69 us
    unnamed x21, local copies, waits for them, and re-layouts  3.35 us
    dot_general x1, matrix products, per_device(): lax.dot_general(dup, x, tn, preferred_element_type=f32).astype(jnp.bfloat16)  2.97 us

profile of v2, /device:TPU:0, one launch (start us, length us, event | category | flops | bytes accessed | tf_op | source)
XLA Modules:
  0.0 130.5 jit_solution(11569218448676985583)
XLA Ops:
  0.6 0.0 copy-start
  0.7 1.4 %copy-done = bf16[2,192,2048]{2,1,0:T(8,128)(2,1)S(1)} copy-done((bf16[2,192,2048]{2,1,0:T(8,128)(2,1)S(1)}, bf16[2,192,2048]{2,1,0:T(8,128)(2,1)}, u32[]{:S(2)}) %copy-start) | copy-done | bytes 1572888
  2.0 0.7 fusion.9
  2.8 0.1 copy.23
  2.9 0.6 pad.8.tab_ref
  3.5 51.6 %shard_map.110 = (bf16[1024,2048]{1,0:T(8,128)(2,1)}, bf16[1024,2048]{1,0:T(8,128)(2,1)}, bf16[1024,128]{1,0:T(8,128)(2,1)}) custom-call(bf16[128,512]{1,0:T(8,128)(2,1)} %tok_ref.1, bf16[128,512]{1,0:T(8,128)(2,1)} %cot_ref.1, bf16[128,128]{1,0:T(8,128)(2,1)} %pad.8.tab_ref), custom_call_target="tpu_custom_call" | custom-call | tf_op jit(solution)/shard_map/pallas_call | solution.py:164
  55.1 1.1 dynamic-slice_convert_fusion
  56.2 0.2 copy.24
  56.4 4.7 %fusion.12 = f32[1024,384]{0,1:T(8,128)S(1)} fusion(bf16[1024,2048]{1,0:T(8,128)(2,1)} %get-tuple-element.12, bf16[384,2048]{1,0:T(8,128)(2,1)} %bitcast.44), kind=kOutput, calls=%fused_computation.26 | convolution fusion | flops 1610612736 | bytes 7340032 | tf_op jit(solution)/shard_map/dot_general | solution.py:357
  61.1 1.8 %fusion.11 = f32[1024,384]{0,1:T(8,128)S(1)} fusion(bf16[1024,2048]{1,0:T(8,128)(2,1)S(1)} %copy-done.5, bf16[384,2048]{1,0:T(8,128)(2,1)S(1)} %bitcast.42), kind=kOutput, calls=%fused_computation.25 | convolution fusion | flops 1610612736 | bytes 7340032 | tf_op jit(solution)/shard_map/dot_general | solution.py:358
  62.9 0.3 copy-done.1
  63.3 3.7 %multiply_multiply_fusion = (f32[1024,384]{0,1:T(8,128)S(1)}, bf16[1024,384]{0,1:T(8,128)(2,1)}, bf16[1024,384]{0,1:T(8,128)(2,1)S(1)}, bf16[1024,384]{0,1:T(8,128)(2,1)}) fusion(f32[1024,384]{0,1:T(8,128)S(1)} %fusion.11, f32[1024,384]{0,1:T(8,128)S(1)} %fusion.12, f32[1024,2]{0,1:T(2,128)S(1)} %copy.24, bf16[1024,2048]{1,0:T(8,128)(2,1)S(1)} %copy-done.1, ...), kind=kOutput, calls=%fused_computation.17 | convolution fusion | flops 1617690624 | bytes 12853248 | tf_op jit(solution)/shard_map/dot_general | solution.py:359
  66.9 3.0 %convolution_convert_fusion.1 = bf16[384,2048]{1,0:T(8,128)(2,1)} fusion(bf16[1024,384]{0,1:T(8,128)(2,1)S(1)} %get-tuple-element.17, bf16[1024,2048]{1,0:T(8,128)(2,1)S(1)} %copy-done.1), kind=kOutput, calls=%fused_computation.4 | convolution fusion | flops 1611399168 | bytes 6553600 | tf_op jit(solution)/shard_map/dot_general | solution.py:394
  69.9 0.1 reduce_sum.40
  70.0 0.6 pad.9.score
  70.6 5.5 %convolution_convert_fusion.3 = bf16[384,2048]{1,0:T(8,128)(2,1)} fusion(bf16[1024,384]{0,1:T(8,128)(2,1)} %get-tuple-element.16, bf16[1024,2048]{1,0:T(8,128)(2,1)} %get-tuple-element.12), kind=kOutput, calls=%fused_computation.6 | convolution fusion | flops 1611399168 | bytes 6553600 | tf_op jit(solution)/shard_map/dot_general | solution.py:392
  76.2 0.0 copy-start.8
  76.2 0.0 copy-start.9
  76.2 3.0 %convolution_convert_fusion.2 = bf16[384,2048]{1,0:T(8,128)(2,1)} fusion(bf16[1024,384]{0,1:T(8,128)(2,1)S(1)} %copy-done.3, bf16[1024,2048]{1,0:T(8,128)(2,1)S(1)} %copy-done.6), kind=kOutput, calls=%fused_computation.5 | convolution fusion | flops 1611399168 | bytes 6553600 | tf_op jit(solution)/shard_map/dot_general | solution.py:393
  79.2 5.3 %convolution_convert_fusion = bf16[1024,2048]{1,0:T(8,128)(2,1)} fusion(bf16[384,2048]{1,0:T(8,128)(2,1)S(1)} %bitcast.43, bf16[384,2048]{1,0:T(8,128)(2,1)S(1)} %bitcast.45, bf16[1024,384]{0,1:T(8,128)(2,1)S(1)} %copy-done.3, bf16[1024,384]{0,1:T(8,128)(2,1)S(1)} %copy-done.2), kind=kOutput, calls=%fused_computation | convolution fusion | flops 3232759808 | bytes 8912896 | tf_op jit(solution)/shard_map/dot_general | solution.py:368
  84.4 43.0 %shard_map.111 = (bf16[128,512]{1,0:T(8,128)(2,1)}, f32[32,8,128]{2,1,0:T(8,128)}) custom-call(bf16[4,2,128,2048]{3,2,1,0:T(8,128)(2,1)} %bitcast.39, f32[8,8,128]{2,1,0:T(8,128)} %pad.9.score), custom_call_target="tpu_custom_call" | custom-call | tf_op jit(solution)/shard_map/pallas_call | solution.py:298
  127.4 0.9 bitcast_reduce_fusion
  128.4 0.6 select_reduce_fusion
  129.0 1.6 %copy.27 = bf16[128,512]{1,0:T(8,128)(2,1)} copy(bf16[128,512]{1,0:T(8,128)(2,1)} %get-tuple-element.24) | data formatting | bytes 262144
  (15 shorter events, 0.0 us)
Async XLA Ops:
  0.6 1.4 %copy-start = (bf16[2,192,2048]{2,1,0:T(8,128)(2,1)S(1)}, bf16[2,192,2048]{2,1,0:T(8,128)(2,1)}, u32[]{:S(2)}) copy-start(bf16[2,192,2048]{2,1,0:T(8,128)(2,1)} %param.13) | copy-start | bytes 4718596
  56.4 4.7 %copy-start.5 = (bf16[1024,2048]{1,0:T(8,128)(2,1)S(1)}, bf16[1024,2048]{1,0:T(8,128)(2,1)}, u32[]{:S(2)}) copy-start(bf16[1024,2048]{1,0:T(8,128)(2,1)} %get-tuple-element.12) | copy-start | bytes 12582916
  56.4 4.7 %copy-start.7 = (bf16[2,192,2048]{2,1,0:T(8,128)(2,1)S(1)}, bf16[2,192,2048]{2,1,0:T(8,128)(2,1)}, u32[]{:S(2)}) copy-start(bf16[2,192,2048]{2,1,0:T(8,128)(2,1)} %param.12) | copy-start | bytes 4718596
  61.1 2.2 %copy-start.1 = (bf16[1024,2048]{1,0:T(8,128)(2,1)S(1)}, bf16[1024,2048]{1,0:T(8,128)(2,1)}, u32[]{:S(2)}) copy-start(bf16[1024,2048]{1,0:T(8,128)(2,1)} %get-tuple-element.11) | copy-start | bytes 12582916
  70.6 5.5 %copy-start.3 = (bf16[1024,384]{0,1:T(8,128)(2,1)S(1)}, bf16[1024,384]{0,1:T(8,128)(2,1)}, u32[]{:S(2)}) copy-start(bf16[1024,384]{0,1:T(8,128)(2,1)} %get-tuple-element.18) | copy-start | bytes 2359300
  70.6 5.5 %copy-start.6 = (bf16[1024,2048]{1,0:T(8,128)(2,1)S(1)}, bf16[1024,2048]{1,0:T(8,128)(2,1)}, u32[]{:S(2)}) copy-start(bf16[1024,2048]{1,0:T(8,128)(2,1)} %get-tuple-element.12) | copy-start | bytes 12582916
  76.2 3.0 %copy-start.2 = (bf16[1024,384]{0,1:T(8,128)(2,1)S(1)}, bf16[1024,384]{0,1:T(8,128)(2,1)}, u32[]{:S(2)}) copy-start(bf16[1024,384]{0,1:T(8,128)(2,1)} %get-tuple-element.16) | copy-start | bytes 2359300
  76.2 3.0 %copy-start.8 = (bf16[2,192,2048]{2,1,0:T(8,128)(2,1)S(1)}, bf16[2,192,2048]{2,1,0:T(8,128)(2,1)}, u32[]{:S(2)}) copy-start(bf16[2,192,2048]{2,1,0:T(8,128)(2,1)} %param.12) | copy-start | bytes 4718596
  76.2 3.0 %copy-start.9 = (bf16[2,192,2048]{2,1,0:T(8,128)(2,1)S(1)}, bf16[2,192,2048]{2,1,0:T(8,128)(2,1)}, u32[]{:S(2)}) copy-start(bf16[2,192,2048]{2,1,0:T(8,128)(2,1)} %param.11) | copy-start | bytes 4718596
  84.4 43.9 %copy-start.4 = (s32[128,8]{0,1:T(8,128)S(1)}, s32[128,8]{0,1:T(8,128)}, u32[]{:S(2)}) copy-start(s32[128,8]{0,1:T(8,128)} %param.9) | copy-start | bytes 12292
